TPU v7x, 32 devices: a whole 2x2x4 slice. The times are simulated.
32 devices in a mesh: space: 32 (over z, y, x, core), mem: 1.
Axes of the slice: x: 2, y: 2, z: 4, core: 2. Of those that a mesh axis runs over, the one named last changes fastest.
Arguments:
- members: bfloat16 [128, 768, 2, 384], P(('space', 'mem')), may hold values from -6 to 6
- state: float32 [768, 2, 384], P('space'), may hold values from -6 to 6
- cotangent: float32 [768, 2, 384], P('space'), may hold values from -6 to 6
- conv_in: float32 [3, 3, 128, 2], replicated, may hold values from -1.5 to 1.5
- conv_out: float32 [3, 3, 2, 128], replicated, may hold values from -0.1875 to 0.1875
- bias: float32 [128], replicated, may hold values from -3 to 3
Outputs:
- increment: float32 [768, 2, 384], P('space')
- response: float32 [768, 2, 384], P('space')
All inputs are finite; a program needn't handle non-finite values.
Results may differ from a plain program's by a relative error of at most 0.0045.
Values may be sent and summed in bfloat16 or wider, within the bound.
A program may use at most 64 MiB of HBM per device.

v0:
```python
import functools

import jax
import jax.numpy as jnp
from jax import lax
from jax.experimental import pallas as pl
from jax.experimental.pallas import tpu as pltpu
from jax.sharding import PartitionSpec as P

HALF = 16


def flip(index, stride):
    return index + stride * (1 - 2 * lax.rem(index // stride, 2))


def flip_all(index, mask):
    stride = 1
    while stride <= mask:
        if mask & stride:
            index = flip(index, stride)
        stride *= 2
    return index


def stages_of(count):
    held = [0]
    steps = []
    stride = count // 2
    while stride >= 8:
        steps.append([(stride, list(held))])
        held = held + [m ^ stride for m in held]
        stride //= 2
    half = max(1, len(held) // 2)
    first, second = held[:half], held[half:]
    steps.append([(2, first), (4, second)])
    first = first + [m ^ 2 for m in first]
    second = second + [m ^ 4 for m in second]
    steps.append([(4, first), (2, second)])
    return steps


def greet(me, count, extra=()):
    barrier = pltpu.get_barrier_semaphore()
    friends = list(extra)
    stride = 1
    while stride < count:
        friends.append(flip(me, stride))
        stride *= 2
    for friend in friends:
        pl.semaphore_signal(
            barrier, inc=1, device_id={"space": friend}, device_id_type=pl.DeviceIdType.MESH
        )
    pl.semaphore_wait(barrier, len(friends))


def gather_kernel(count, block_ref, whole_ref, send_sem, recv_sem):
    me = lax.axis_index("space")
    greet(me, count)

    def remote(mask, stride):
        owner = flip_all(me, mask)
        source = block_ref if mask == 0 else whole_ref.at[owner]
        slot = mask ^ stride
        return pltpu.make_async_remote_copy(
            src_ref=source,
            dst_ref=whole_ref.at[owner],
            send_sem=send_sem.at[slot],
            recv_sem=recv_sem.at[slot],
            device_id={"space": flip(me, stride)},
            device_id_type=pl.DeviceIdType.MESH,
        )

    started = []
    pair = []
    for step in stages_of(count):
        now = []
        for position in range(max(len(masks) for stride, masks in step)):
            for stride, masks in step:
                if position < len(masks):
                    copy = remote(masks[position], stride)
                    copy.start()
                    now.append((copy, masks[position] ^ stride))
        if not pair:
            copy = remote(0, 1)
            copy.start()
            pair.append(copy)
            whole_ref[me] = block_ref[...]
        for copy, mask in now:
            copy.wait_recv()
            other = remote(mask, 1)
            other.start()
            pair.append(other)
            started.append(copy)
    for copy in started:
        copy.wait_send()
    for copy in pair:
        copy.wait()


def gather(block):
    count = lax.axis_size("space")
    return pl.pallas_call(
        functools.partial(gather_kernel, count),
        out_shape=jax.ShapeDtypeStruct((count,) + block.shape, block.dtype),
        in_specs=[pl.BlockSpec(memory_space=pltpu.VMEM)],
        out_specs=pl.BlockSpec(memory_space=pltpu.VMEM),
        scratch_shapes=[
            pltpu.SemaphoreType.DMA((count,)),
            pltpu.SemaphoreType.DMA((count,)),
        ],
        compiler_params=pltpu.CompilerParams(collective_id=0, has_side_effects=True),
        name="gather",
    )(block)


def scatter_kernel(
    count, rim, part_ref, sum_ref, left_ref, right_ref,
    out_buf, in_buf, edge_buf, send_sem, recv_sem, edge_send, edge_recv,
):
    me = lax.axis_index("space")
    before, after = lax.rem(me + count - 1, count), lax.rem(me + 1, count)
    greet(me, count, (before, after))
    arrived = {mask: [] for mask in range(count)}

    def value(mask):
        total = part_ref[flip_all(me, mask)]
        for slot in arrived[mask]:
            total = total + in_buf[slot].astype(jnp.float32)
        return total

    sent = []
    for step in [[(1, list(range(0, count, 2)))]] + stages_of(count)[::-1]:
        now = []
        for position in range(max(len(masks) for stride, masks in step)):
            for stride, masks in step:
                if position < len(masks):
                    slot = masks[position] ^ stride
                    out_buf[slot] = value(slot).astype(out_buf.dtype)
                    copy = pltpu.make_async_remote_copy(
                        src_ref=out_buf.at[slot],
                        dst_ref=in_buf.at[slot],
                        send_sem=send_sem.at[slot],
                        recv_sem=recv_sem.at[slot],
                        device_id={"space": flip(me, stride)},
                        device_id_type=pl.DeviceIdType.MESH,
                    )
                    copy.start()
                    now.append((copy, masks[position], slot))
        for copy, mask, slot in now:
            copy.wait_recv()
            arrived[mask].append(slot)
            sent.append(copy)
    total = value(0)
    sum_ref[...] = total
    edge_buf[0] = total[:rim]
    edge_buf[1] = total[total.shape[0] - rim :]
    edges = [
        pltpu.make_async_remote_copy(
            src_ref=edge_buf.at[side],
            dst_ref=target,
            send_sem=edge_send.at[side],
            recv_sem=edge_recv.at[side],
            device_id={"space": friend},
            device_id_type=pl.DeviceIdType.MESH,
        )
        for side, target, friend in ((0, right_ref, before), (1, left_ref, after))
    ]
    for copy in edges:
        copy.start()
    for copy in sent:
        copy.wait_send()
    for copy in edges:
        copy.wait()


def scatter(parts, rim):
    count, rows, lat_count = parts.shape
    return pl.pallas_call(
        functools.partial(scatter_kernel, count, rim),
        out_shape=(
            jax.ShapeDtypeStruct((rows, lat_count), jnp.float32),
            jax.ShapeDtypeStruct((rim, lat_count), jnp.float32),
            jax.ShapeDtypeStruct((rim, lat_count), jnp.float32),
        ),
        in_specs=[pl.BlockSpec(memory_space=pltpu.VMEM)],
        out_specs=(pl.BlockSpec(memory_space=pltpu.VMEM),) * 3,
        scratch_shapes=[
            pltpu.VMEM((count, rows, lat_count), jnp.bfloat16),
            pltpu.VMEM((count, rows, lat_count), jnp.bfloat16),
            pltpu.VMEM((2, rim, lat_count), jnp.float32),
            pltpu.SemaphoreType.DMA((count,)),
            pltpu.SemaphoreType.DMA((count,)),
            pltpu.SemaphoreType.DMA((2,)),
            pltpu.SemaphoreType.DMA((2,)),
        ],
        compiler_params=pltpu.CompilerParams(collective_id=1, has_side_effects=True),
        name="scatter",
    )(parts)


def covariance_kernel(members_ref, whole_ref, lat_ref, lon_ref, sum_ref, banded_ref):
    lat_count = lat_ref.shape[0]

    @pl.when(pl.program_id(0) == 0)
    def _():
        sum_ref[...] = jnp.zeros_like(sum_ref)

    for start in range(0, whole_ref.shape[1], lat_count):
        columns = slice(start, start + lat_count)
        product = members_ref[0, :, columns].astype(jnp.float32) * whole_ref[:, columns].astype(
            jnp.float32
        )
        banded_ref[:, columns] = jnp.dot(
            product.astype(jnp.bfloat16), lat_ref[...], preferred_element_type=jnp.float32
        ).astype(jnp.bfloat16)
    for start in range(0, whole_ref.shape[1], lat_count):
        columns = slice(start, start + lat_count)
        spread = jnp.dot(
            lon_ref[...], banded_ref[:, columns], preferred_element_type=jnp.float32
        )
        sum_ref[:, columns] += members_ref[0, :, columns].astype(jnp.float32) * spread


def covariance(members, whole, lat_loc, lon_loc):
    count, lon_count, width = members.shape
    return pl.pallas_call(
        covariance_kernel,
        grid=(count,),
        out_shape=jax.ShapeDtypeStruct((lon_count, width), jnp.float32),
        in_specs=[
            pl.BlockSpec((1, lon_count, width), lambda m: (m, 0, 0)),
            pl.BlockSpec(whole.shape, lambda m: (0, 0)),
            pl.BlockSpec(lat_loc.shape, lambda m: (0, 0)),
            pl.BlockSpec(lon_loc.shape, lambda m: (0, 0)),
        ],
        out_specs=pl.BlockSpec((lon_count, width), lambda m: (0, 0)),
        scratch_shapes=[pltpu.VMEM((lon_count, width), jnp.bfloat16)],
        name="covariance",
    )(members, whole, lat_loc, lon_loc)


def padded_2(cells, axis, width):
    count = lax.axis_size(axis)
    head = cells[:width]
    tail = cells[cells.shape[0] - width :]
    return jnp.concatenate(
        [
            lax.ppermute(tail, axis, [(i, (i + 1) % count) for i in range(count)]),
            cells,
            lax.ppermute(head, axis, [((i + 1) % count, i) for i in range(count)]),
        ],
        axis=0,
    )


def convolve(padded, weight, precision=None):
    row_count = padded.shape[0] - 2
    lat_count = padded.shape[2]
    out_count = weight.shape[2]
    in_count = weight.shape[3]
    if precision is None:
        padded = padded.astype(jnp.bfloat16)
        weight = weight.astype(jnp.bfloat16)
    if out_count <= in_count:
        flattened = weight.reshape(9 * out_count, in_count)
        product = jnp.einsum(
            "kc,xcy->xky", flattened, padded, preferred_element_type=jnp.float32
        )
        product = jnp.pad(product, ((0, 0), (0, 0), (1, 1)))
        summed = jnp.zeros((row_count, out_count, lat_count), jnp.float32)
        for step_lon in range(3):
            for step_lat in range(3):
                tap_index = step_lon * 3 + step_lat
                summed = (
                    summed
                    + product[
                        step_lon : step_lon + row_count,
                        tap_index * out_count : (tap_index + 1) * out_count,
                        step_lat : step_lat + lat_count,
                    ]
                )
        return summed
    lat_padded = jnp.pad(padded, ((0, 0), (0, 0), (1, 1)))
    stacked = jnp.concatenate(
        [
            lat_padded[step_lon : step_lon + row_count, :, step_lat : step_lat + lat_count]
            for step_lon in range(3)
            for step_lat in range(3)
        ],
        axis=1,
    )
    flattened = jnp.transpose(weight, (2, 0, 1, 3)).reshape(out_count, 9 * in_count)
    return jnp.einsum(
        "ok,xky->xoy", flattened, stacked, precision=precision, preferred_element_type=jnp.float32
    )


def split(values):
    high = lax.reduce_precision(values, 8, 7)
    return high.astype(jnp.bfloat16), (values - high).astype(jnp.bfloat16)


def convolve_fine(padded, weight):
    out_count, in_count = weight.shape[2:]
    upper, lower = split(padded)
    weight_upper, weight_lower = split(weight)
    if out_count <= in_count:
        both = jnp.concatenate([upper, lower], axis=1)
        stacked = jnp.concatenate([weight_upper, weight_lower], axis=2)
        stacked = jnp.concatenate([stacked, stacked], axis=3)
        result = convolve(both, stacked)
        return result[:, :out_count] + result[:, out_count:]
    return convolve(padded, weight, lax.Precision.HIGH)


def flipped(weight):
    return jnp.transpose(weight[::-1, ::-1], (0, 1, 3, 2))


def band_matrix(count, wrap):
    row_index = jnp.arange(count)[:, None]
    col_index = jnp.arange(count)[None, :]
    distance = jnp.abs(row_index - col_index)
    if wrap:
        distance = jnp.minimum(distance, count - distance)
    ratio = distance.astype(jnp.float32) / (HALF + 1.0)
    return jnp.where(distance <= HALF, 1.0 - ratio * ratio, 0.0).astype(jnp.bfloat16)


def per_device(members, state, cotangent, conv_in, conv_out, bias):
    row_count, var_count, lat_count = state.shape
    count = lax.axis_size("space")
    direct = count >= 8 and count & (count - 1) == 0
    rim_width = 2
    joined = jnp.concatenate([state, cotangent], axis=1)
    padded = padded_2(joined, "space", rim_width)
    state_pad = padded[:, :var_count]
    cot_pad = padded[:, var_count:]
    activity = jnp.tanh(convolve_fine(state_pad, conv_in) + bias[None, :, None])
    slopes = 1.0 - activity * activity
    backward = slopes * convolve_fine(cot_pad, flipped(conv_out))
    gradient = cotangent + convolve_fine(backward, flipped(conv_in))
    gradient = gradient.astype(jnp.bfloat16)
    width = var_count * lat_count
    gradient = gradient.reshape(row_count, width)
    if direct:
        whole = gather(gradient).reshape(count * row_count, width)
    else:
        whole = lax.all_gather(gradient, "space", axis=0, tiled=True)
    merged = members.reshape(members.shape[0], members.shape[1], width)
    lat_loc = band_matrix(lat_count, False)
    lon_loc = band_matrix(merged.shape[1], True)
    contrib = covariance(merged, whole, lat_loc, lon_loc)
    member_count = members.shape[0] * lax.axis_size("space") * lax.axis_size("mem")
    if direct:
        own, left, right = scatter(
            contrib.reshape(count, row_count, width), rim_width
        )
        total = jnp.concatenate([left, own, right], axis=0)
        total = total.reshape(row_count + 2 * rim_width, var_count, lat_count)
        if lax.axis_size("mem") > 1:
            total = lax.psum(total, "mem")
        incr_pad = total / (member_count - 1.0)
        increment = incr_pad[rim_width : rim_width + row_count]
    else:
        member_sum = lax.psum(contrib, "mem")
        block_sum = lax.psum_scatter(member_sum, "space", scatter_dimension=0, tiled=True)
        increment = block_sum.reshape(state.shape) / (member_count - 1.0)
        incr_pad = padded_2(increment, "space", rim_width)
    tangent_hidden = slopes * convolve(incr_pad, conv_in)
    response = increment + convolve(tangent_hidden, conv_out)
    return (increment, response)


def solution(mesh):
    in_specs = (
        P(("space", "mem"), None, None, None),
        P("space", None, None),
        P("space", None, None),
        P(),
        P(),
        P(),
    )
    out_specs = (P("space", None, None), P("space", None, None))
    return jax.shard_map(
        per_device, mesh=mesh, in_specs=in_specs, out_specs=out_specs, check_vma=False
    )
```

profile of v0, /device:TPU:0, one launch (start us, length us, event | category | flops | bytes accessed | tf_op | source)
XLA Modules:
  0.0 104.1 jit_solution(17729614231557913497)
XLA Ops:
  0.6 0.8 pad_maximum_fusion.3
  1.4 0.5 collective-permute-start
  1.9 6.0 %collective-permute-start.1 = (f32[2,4,384]{2,1,0:T(4,128)S(1)}, f32[2,4,384]{2,1,0:T(4,128)S(1)}, u32[]{:S(2)}, u32[]{:S(2)}) collective-permute-start(f32[2,4,384]{2,1,0:T(4,128)S(1)} %get-tuple-element.21), channel_id=1, source_target_pairs={{1,0},{2,1},{3,2},{4,3},{5,4},{6,5},{7,6},{8,7},{9,8},{10,9},{11,1... | collective-permute-start | bytes 36872 | tf_op jit(solution)/shard_map/ppermute | solution.py:251
  7.9 1.8 %select_convert_fusion.lon_ref = bf16[768,768]{1,0:T(8,128)(2,1)} fusion(), kind=kLoop, calls=%fused_computation.20 | loop fusion | flops 6488064 | bytes 1179648 | tf_op jit(solution)/shard_map/convert_element_type | solution.py:328
  9.7 0.8 select_convert_fusion.1.lat_ref
  10.5 0.7 reduce-precision_convert_fusion.1
  11.2 0.7 convert_bitcast_fusion
  11.9 0.8 fusion.47
  12.7 0.7 reshape.49
  13.5 0.0 copy-start
  13.5 0.0 copy-start.1
  13.5 11.4 %reshape.40.members_ref = bf16[4,768,768]{2,1,0:T(8,128)(2,1)} reshape(bf16[4,768,2,384]{3,2,1,0:T(2,128)(2,1)} %param.6) | data formatting | bytes 9437184 | tf_op jit(solution)/shard_map/reshape | solution.py:351
  25.0 0.0 collective-permute-done
  25.0 0.0 collective-permute-done.1
  25.0 0.0 copy-done
  25.0 0.0 copy-done.1
  25.0 0.1 pad_maximum_fusion
  25.1 0.1 fusion.43
  25.2 0.1 fusion.42
  25.2 1.1 %pad_slice_fusion.12 = (f32[26,2,384]{2,1,0:T(2,128)S(1)}, f32[26,2,384]{2,1,0:T(2,128)S(1)}, f32[26,2,384]{2,1,0:T(2,128)S(1)}, f32[26,2,384]{2,1,0:T(2,128)S(1...) fusion(f32[28,2,384]{2,1,0:T(2,128)S(1)} %get-tuple-element.12,, ...), kind=kLoop, calls=%fused_computation.57 | loop fusion | bytes 1130496 | tf_op jit(solution)/shard_map/slice | solution.py:287
  26.3 0.1 pad_maximum_fusion.1
  26.4 0.1 fusion.44
  26.5 0.8 concatenate.39
  27.3 0.0 copy-start.3
  27.3 4.5 %fusion.48 = f32[26,384,128]{1,2,0:T(8,128)} fusion(f32[26,18,384]{2,1,0:T(8,128)S(1)} %concatenate.39, f32[128,18,1]{0,1,2:T(8,128)S(1)} %reshape.49), kind=kOutput, calls=%fused_computation.92 | convolution fusion | flops 138018816 | bytes 5839872 | tf_op jit(solution)/shard_map/ok,xky->xoy/dot_general | solution.py:294
  31.8 0.8 concatenate.40
  32.5 0.0 copy-done.3
  32.5 6.1 %reduce-precision_convert_fusion = (bf16[26,128,384]{2,1,0:T(8,128)(2,1)S(1)}, bf16[26,128,384]{2,1,0:T(8,128)(2,1)S(1)}) fusion(f32[26,18,384]{2,1,0:T(8,128)S(1)} %concatenate.40, f32[128,18,1]{0,1,2:T(8,128)S(1)} %reshape.50, f32[26,384,128]{1,2,0:T(8,128)} %fusion.48, f32[128]{0:T(128)S(1)} %copy-done.3), kind=kOutput, calls=%fused_computation.1 | convolution fusion | flops 148242432 | bytes 10952192 | tf_op jit(solution)/shard_map/ok,xky->xoy/dot_general | solution.py:294
  38.6 1.1 %fusion.12 = f32[26,36,384]{2,1,0:T(8,128)S(1)} fusion(bf16[36,256,1]{1,0,2:T(8,128)(2,1)S(1)} %reshape.51, bf16[26,128,384]{2,1,0:T(8,128)(2,1)S(1)} %get-tuple-element.9, bf16[26,128,384]{2,1,0:T(8,128)(2,1)S(1)} %get-tuple-element.8), kind=kOutput, calls=%fused_computation.28 | convolution fusion | flops 194248704 | bytes 6567936 | tf_op jit(solution)/shard_map/kc,xcy->xky/dot_general | solution.py:267
  39.8 0.5 fusion.26
  40.3 0.1 fusion.37
  40.4 0.6 copy.8
  41.0 19.2 %gather.1 = bf16[32,24,768]{2,1,0:T(8,128)(2,1)} custom-call(bf16[24,768]{1,0:T(8,128)(2,1)} %bitcast.40), custom_call_target="tpu_custom_call" | custom-call | tf_op jit(solution)/shard_map/gather/pallas_call | solution.py:103
  60.2 12.3 %covariance.1 = f32[768,768]{1,0:T(8,128)} custom-call(bf16[4,768,768]{2,1,0:T(8,128)(2,1)} %reshape.40.members_ref, bf16[768,768]{1,0:T(8,128)(2,1)} %bitcast.39, bf16[384,384]{1,0:T(8,128)(2,1)} %select_convert_fusion.1.lat_ref, bf16[768,768]{1,0:T(8,128)(2,1)} %select_convert_fusion.lon_ref), custom_call_target="tpu_custom_call" | custom-call | tf_op jit(solution)/shard_map/covariance/pallas_call | solution.py:227
  72.5 24.1 %scatter.1 = (f32[24,768]{1,0:T(8,128)}, f32[2,768]{1,0:T(2,128)}, f32[2,768]{1,0:T(2,128)}) custom-call(f32[32,24,768]{2,1,0:T(8,128)} %bitcast.38), custom_call_target="tpu_custom_call" | custom-call | tf_op jit(solution)/shard_map/scatter/pallas_call | solution.py:179
  96.6 0.9 fusion.41
  97.6 0.3 pad_slice_fusion.24
  98.2 0.0 copy-start.2
  98.2 0.8 concatenate.45
  99.0 3.9 %fusion.15 = f32[26,18,384]{2,1,0:T(8,128)S(1)} fusion(bf16[18,128,1]{1,0,2:T(8,128)(2,1)S(1)} %reshape.53, f32[26,384,128]{1,2,0:T(8,128)} %fusion.48, f32[128]{0:T(128)S(1)} %copy-done.3, bf16[26,18,384]{2,1,0:T(8,128)(2,1)S(1)} %concatenate.45, bf16[128,18,1]{0,1,2:T(8,128)(2,1)S(1)} %reshape.52), kind=kOutput, calls=%fused_computation.29 | convolution fusion | flops 98402304 | bytes 6199808 | tf_op jit(solution)/shard_map/kc,xcy->xky/dot_general | solution.py:267
  102.9 0.0 copy-done.2
  102.9 1.2 %fusion.33 = f32[24,2,384]{2,1,0:T(2,128)} fusion(f32[24,2,384]{2,1,0:T(2,128)S(1)} %slice.227, f32[26,18,384]{2,1,0:T(8,128)S(1)} %fusion.15), kind=kLoop, calls=%fused_computation.51 | loop fusion | flops 165888 | bytes 1327104 | tf_op jit(solution)/shard_map/add | solution.py:372
  (12 shorter events, 0.3 us)
Async XLA Ops:
  1.4 23.6 %collective-permute-start = (f32[2,4,384]{2,1,0:T(4,128)S(1)}, f32[2,4,384]{2,1,0:T(4,128)S(1)}, u32[]{:S(2)}, u32[]{:S(2)}) collective-permute-start(f32[2,4,384]{2,1,0:T(4,128)S(1)} %get-tuple-element.20), channel_id=1, source_target_pairs={{0,1},{1,2},{2,3},{3,4},{4,5},{5,6},{6,7},{7,8},{8,9},{9,10},{10,1... | collective-permute-start | bytes 36872 | tf_op jit(solution)/shard_map/ppermute | solution.py:249
  1.9 23.0 %collective-permute-start.1 = (f32[2,4,384]{2,1,0:T(4,128)S(1)}, f32[2,4,384]{2,1,0:T(4,128)S(1)}, u32[]{:S(2)}, u32[]{:S(2)}) collective-permute-start(f32[2,4,384]{2,1,0:T(4,128)S(1)} %get-tuple-element.21), channel_id=1, source_target_pairs={{1,0},{2,1},{3,2},{4,3},{5,4},{6,5},{7,6},{8,7},{9,8},{10,9},{11,1... | collective-permute-start | bytes 36872 | tf_op jit(solution)/shard_map/ppermute | solution.py:251
  13.5 11.5 %copy-start = (f32[24,2,384]{2,1,0:T(2,128)S(1)}, f32[24,2,384]{2,1,0:T(2,128)}, u32[]{:S(2)}) copy-start(f32[24,2,384]{2,1,0:T(2,128)} %param.8) | copy-start | bytes 221188
  13.5 11.5 %copy-start.1 = (f32[24,2,384]{2,1,0:T(2,128)S(1)}, f32[24,2,384]{2,1,0:T(2,128)}, u32[]{:S(2)}) copy-start(f32[24,2,384]{2,1,0:T(2,128)} %param.7) | copy-start | bytes 221188
  27.3 5.2 %copy-start.3 = (f32[128]{0:T(128)S(1)}, f32[128]{0:T(128)}, u32[]{:S(2)}) copy-start(f32[128]{0:T(128)} %param.11) | copy-start | bytes 1540
  98.2 4.7 %copy-start.2 = (f32[24,2,384]{2,1,0:T(2,128)}, f32[24,2,384]{2,1,0:T(2,128)S(1)}, u32[]{:S(2)}) copy-start(f32[24,2,384]{2,1,0:T(2,128)S(1)} %slice.227) | copy-start | bytes 221188
where the time goes:
time: 105 us; the launch traced here: 104 us
  Pallas kernels  55.6 us (53%)
  local copies, waits for them, and re-layouts  17 us (16%)
  matrix products  15.6 us (15%)
  other arithmetic  8.45 us (8%)
  starting transfers between devices  6.52 us (6%)
    pallas_call x1, Pallas kernels, scatter(): pl.pallas_call(functools.partial(scatter_kernel, count, rim), out_shape=(...  24.1 us
    pallas_call x1, Pallas kernels, gather(): pl.pallas_call(functools.partial(gather_kernel, count), out_shape=jax.Sha...  19.2 us
    pallas_call x1, Pallas kernels, covariance(): pl.pallas_call(covariance_kernel, grid=(count,), out_shape=jax.ShapeDtype...  12.3 us
    reshape x1, local copies, waits for them, and re-layouts, per_device(): merged = members.reshape(members.shape[0], members.shape[1], width)  11.4 us
    dot_general x2, matrix products, convolve(): jnp.einsum('ok,xky->xoy', flattened, stacked, precision=precision, prefer...  10.5 us
    ppermute x1, starting transfers between devices, padded_2(): lax.ppermute(head, axis, [((i + 1) % count, i) for i in range(count)])  5.97 us
    dot_general x2, matrix products, convolve(): jnp.einsum('kc,xcy->xky', flattened, padded, preferred_element_type=jnp.f...  5.03 us
    convert_element_type x2, other arithmetic, band_matrix(): jnp.where(distance <= HALF, 1.0 - ratio * ratio, 0.0).astype(jnp.bfloat16)  2.62 us
  transfers between devices with their start and end apart: 2, of which 0 were waited for; matrix products, arithmetic and copies ran while one was open for 16% of the time, Pallas kernels for 0%

commit v1 on v0

--- a/solution.py
+++ b/solution.py
@@ -8,6 +8,7 @@
 from jax.sharding import PartitionSpec as P
 
 HALF = 16
+LANES = 128
 
 
 def flip(index, stride):
@@ -328,8 +329,580 @@
     return jnp.where(distance <= HALF, 1.0 - ratio * ratio, 0.0).astype(jnp.bfloat16)
 
 
+def tile_cols(t):
+    return slice(t * LANES, (t + 1) * LANES)
+
+
+def shifted(values, step):
+    if step == 1:
+        return values
+    width = values.shape[-1]
+    column = lax.broadcasted_iota(jnp.int32, values.shape, values.ndim - 1)
+    if step == 0:
+        return jnp.where(column == 0, 0.0, pltpu.roll(values, 1, values.ndim - 1))
+    return jnp.where(column == width - 1, 0.0, pltpu.roll(values, width - 1, values.ndim - 1))
+
+
+def tap_of(distance):
+    ratio = distance / (HALF + 1.0)
+    return jnp.where(distance <= HALF, 1.0 - ratio * ratio, 0.0)
+
+
+def halves(values):
+    high = values.astype(jnp.bfloat16)
+    return high, (values - high.astype(jnp.float32)).astype(jnp.bfloat16)
+
+
+def step_kernel(
+    count, total_members,
+    members_hbm, state_hbm, cot_hbm, win_hbm, wout_hbm, bias_hbm,
+    incr_hbm, resp_hbm,
+    mem_ref, own_ref, halo_ref, taps_ref, wraw_ref, bias_ref, slot_ref,
+    w_state, w_cot, v_in, w_tail, v_tail,
+    slopes_ref, part_ref, q_ref, g_ref, whole_ref, lat_ref, lon_ref, banded_ref, contrib_ref,
+    out_buf, in_buf, total_ref, stage_ref,
+    mem_sem, own_sem, small_sem, halo_send, halo_recv, g_send, g_recv, r_send, r_recv, out_sem,
+):
+    me = lax.axis_index("space")
+    members, lane_tiles, lons, var_count, _ = mem_ref.shape
+    rows = own_ref.shape[2]
+    two = rows * var_count
+    lats = lane_tiles * LANES
+    hidden = slot_ref.shape[2]
+    depth = count // 8
+    before, after = lax.rem(me + count - 1, count), lax.rem(me + 1, count)
+
+    own_loads = []
+    for index, source in enumerate((state_hbm, cot_hbm)):
+        for t in range(lane_tiles):
+            copy = pltpu.make_async_copy(
+                source.at[:, :, tile_cols(t)], own_ref.at[index, t], own_sem.at[index, t]
+            )
+            copy.start()
+            own_loads.append(copy)
+    small_loads = [
+        pltpu.make_async_copy(win_hbm, wraw_ref.at[0], small_sem.at[0]),
+        pltpu.make_async_copy(wout_hbm, wraw_ref.at[1], small_sem.at[1]),
+        pltpu.make_async_copy(bias_hbm, bias_ref, small_sem.at[2]),
+    ]
+    for copy in small_loads:
+        copy.start()
+    mem_loads = []
+    for m in range(members):
+        for t in range(lane_tiles):
+            copy = pltpu.make_async_copy(
+                members_hbm.at[m, :, :, tile_cols(t)], mem_ref.at[m, t], mem_sem.at[m, t]
+            )
+            copy.start()
+            mem_loads.append(copy)
+
+    barrier = pltpu.get_barrier_semaphore()
+    friends = [before, after] + [flip(me, 1), flip(me, 2), flip(me, 4)]
+    friends += [flip_all(me, 8 * j) for j in range(1, depth)]
+    for friend in friends:
+        pl.semaphore_signal(
+            barrier, inc=1, device_id={"space": friend}, device_id_type=pl.DeviceIdType.MESH
+        )
+
+    row = lax.broadcasted_iota(jnp.int32, taps_ref.shape[2:], 0)
+    blank = jnp.where((row & 7) == 6, 1.0, 0.0)
+    for index in range(2):
+        for t in range(lane_tiles):
+            taps_ref[index, t] = blank
+    window = lat_ref.shape[1]
+    for index in range(2):
+        offset = index * (lats - window)
+        y = lax.broadcasted_iota(jnp.int32, (window, window), 0)
+        z = lax.broadcasted_iota(jnp.int32, (window, window), 1)
+        value = tap_of(jnp.abs(y - z).astype(jnp.float32))
+        mine = (z + offset < lats // 2) if index == 0 else (z + offset >= lats // 2)
+        lat_ref[index] = jnp.where(mine, value, 0.0).astype(jnp.bfloat16)
+    i = lax.broadcasted_iota(jnp.int32, lon_ref.shape, 0)
+    j = lax.broadcasted_iota(jnp.int32, lon_ref.shape, 1)
+    gap = i - j + var_count * HALF
+    value = tap_of(jnp.abs(gap).astype(jnp.float32) * 0.5)
+    lon_ref[...] = jnp.where((gap & 1) == 0, value, 0.0).astype(jnp.bfloat16)
+
+    for copy in small_loads:
+        copy.wait()
+    slot_ref[...] = jnp.zeros(slot_ref.shape, jnp.float32)
+    for a in range(3):
+        for b in range(3):
+            place = slice(8 * a + 2 * b, 8 * a + 2 * b + 2)
+            slot_ref[0, place, :] = wraw_ref[0, a, b]
+            slot_ref[1, place, :] = wraw_ref[0, 2 - a, 2 - b]
+            slot_ref[2, place, :] = wraw_ref[1, 2 - a, 2 - b]
+            slot_ref[3, place, :] = wraw_ref[1, a, b]
+    w_tail[...] = slot_ref[0].T.astype(jnp.bfloat16)
+    v_tail[...] = slot_ref[3].astype(jnp.bfloat16)
+    slot_ref[0, 14:15, :] = bias_ref[...]
+    for target, index in ((w_state, 0), (w_cot, 2)):
+        high, low = halves(slot_ref[index].T)
+        target[...] = jnp.concatenate([high, high, low], axis=1)
+    high, low = halves(slot_ref[1])
+    v_in[:32] = jnp.concatenate([high, high], axis=1)
+    v_in[32:] = jnp.concatenate([low, low], axis=1)
+
+    for copy in own_loads:
+        copy.wait()
+    pl.semaphore_wait(barrier, len(friends))
+    edges = []
+    for side, start, friend in ((1, 0, before), (0, rows - 2, after)):
+        copy = pltpu.make_async_remote_copy(
+            src_ref=own_ref.at[:, :, start : start + 2],
+            dst_ref=halo_ref.at[side],
+            send_sem=halo_send.at[side],
+            recv_sem=halo_recv.at[side],
+            device_id={"space": friend},
+            device_id_type=pl.DeviceIdType.MESH,
+        )
+        copy.start()
+        edges.append(copy)
+
+    own_rows = own_ref.reshape(2, lane_tiles, two, LANES)
+    for index in range(2):
+        for c in range(var_count):
+            values = jnp.concatenate(
+                [own_rows[index, t, pl.ds(c, rows, stride=var_count), :] for t in range(lane_tiles)],
+                axis=1,
+            )
+            for b in range(3):
+                moved = shifted(values, b)
+                for t in range(lane_tiles):
+                    taps_ref[index, t, pl.ds(16 + 2 * b + c, rows, stride=8), :] = moved[:, tile_cols(t)]
+
+    def lane_chunks():
+        tiles = [(line, t) for line in range(2) for t in range(lane_tiles)]
+        return [tiles[k : k + 2] for k in range(0, len(tiles), 2)]
+
+    def tap_block(index, j, t):
+        start = pl.multiple_of(8 * j, 8)
+        return taps_ref[index, t, pl.ds(start, 32), :]
+
+    def fine_block(index, j, t):
+        high, low = halves(tap_block(index, j, t))
+        return jnp.concatenate([high, low, high], axis=0)
+
+    def head_pair(p):
+        for chunk in lane_chunks():
+            lines = [(2 * p + line, t) for line, t in chunk]
+            field = jnp.concatenate([fine_block(0, j, t) for j, t in lines], axis=1)
+            misfit = jnp.concatenate([fine_block(1, j, t) for j, t in lines], axis=1)
+            activity = jnp.tanh(jnp.dot(w_state[...], field, preferred_element_type=jnp.float32))
+            slopes = 1.0 - activity * activity
+            back = slopes * jnp.dot(w_cot[...], misfit, preferred_element_type=jnp.float32)
+            high, low = halves(back)
+            pieces = jnp.dot(
+                v_in[...], jnp.concatenate([high, low], axis=0), preferred_element_type=jnp.float32
+            )
+            pieces = pieces[:24] + pieces[32:56]
+            for place, (j, t) in enumerate(lines):
+                slopes_ref[j, :, tile_cols(t)] = slopes[:, tile_cols(place)]
+                part_ref[j, :, tile_cols(t)] = pieces[:, tile_cols(place)]
+
+    pairs = (rows + 2) // 2
+
+    def inner(p, carry):
+        head_pair(p)
+        return carry
+
+    lax.fori_loop(1, pairs - 1, inner, 0)
+
+    for copy in edges:
+        copy.wait()
+    halo_rows = halo_ref.reshape(2, 2, lane_tiles, 2 * var_count, LANES)
+    for side, slot in ((0, 0), (1, rows + 2)):
+        for index in range(2):
+            values = jnp.concatenate(
+                [halo_rows[side, index, t] for t in range(lane_tiles)], axis=1
+            )
+            for b in range(3):
+                moved = shifted(values, b)
+                for line in range(2):
+                    at = 8 * (slot + line) + 2 * b
+                    for t in range(lane_tiles):
+                        taps_ref[index, t, at : at + 2, :] = moved[
+                            2 * line : 2 * line + 2, tile_cols(t)
+                        ]
+
+    def outer(p, carry):
+        head_pair(p * (pairs - 1))
+        return carry
+
+    lax.fori_loop(0, 2, outer, 0)
+
+    def assembled(c):
+        return sum(
+            shifted(tile_rows(q_ref, pl.ds(2 * b + c, rows, stride=8)), b) for b in range(3)
+        )
+
+    def tile_rows(ref, place):
+        return jnp.concatenate([ref[t, place, :] for t in range(lane_tiles)], axis=1)
+
+    def gather_pieces():
+        for t in range(lane_tiles):
+            cols = tile_cols(t)
+            joined = (
+                part_ref[0:rows, 0:8, cols]
+                + part_ref[1 : rows + 1, 8:16, cols]
+                + part_ref[2 : rows + 2, 16:24, cols]
+            )
+            q_ref[t] = joined.reshape(rows * 8, LANES)
+
+    gather_pieces()
+    for c in range(var_count):
+        values = jnp.concatenate(
+            [own_rows[1, t, pl.ds(c, rows, stride=var_count), :] for t in range(lane_tiles)], axis=1
+        )
+        values = values + assembled(c)
+        for t in range(lane_tiles):
+            g_ref[t, pl.ds(c, rows, stride=var_count), :] = values[:, tile_cols(t)]
+    whole_ref[me] = tile_rows(g_ref, slice(None)).astype(jnp.bfloat16)
+
+    forks = [j for j in range(depth) if bin(j).count("1") % 2 == 0]
+    sends = []
+
+    def pass_on(rel, stride):
+        owner = flip_all(me, rel)
+        slot = rel ^ stride
+        copy = pltpu.make_async_remote_copy(
+            src_ref=whole_ref.at[owner],
+            dst_ref=whole_ref.at[owner],
+            send_sem=g_send.at[len(sends)],
+            recv_sem=g_recv.at[slot],
+            device_id={"space": flip_all(me, stride)},
+            device_id_type=pl.DeviceIdType.MESH,
+        )
+        copy.start()
+        sends.append(copy)
+
+    def await_block(rel):
+        owner = flip_all(me, rel)
+        pltpu.make_async_remote_copy(
+            src_ref=whole_ref.at[owner],
+            dst_ref=whole_ref.at[owner],
+            send_sem=g_send.at[0],
+            recv_sem=g_recv.at[rel],
+            device_id={"space": flip(me, 1)},
+            device_id_type=pl.DeviceIdType.MESH,
+        ).wait_recv()
+
+    pass_on(0, 2)
+    pass_on(0, 4)
+    for j in range(1, depth):
+        pass_on(0, 8 * j)
+    pass_on(0, 1)
+    for j in range(depth):
+        if j:
+            await_block(8 * j)
+            pass_on(8 * j, 2)
+            pass_on(8 * j, 4)
+            pass_on(8 * j, 1)
+        if j == 0:
+            for near in (2, 4):
+                await_block(near)
+                if (near == 4) == (j in forks):
+                    pass_on(near, 6 - near)
+                pass_on(near, 1)
+    for j in range(1, depth):
+        for near in (2, 4):
+            rel = 8 * j + near
+            await_block(rel)
+            if (near == 4) == (j in forks):
+                pass_on(rel, 6 - near)
+            pass_on(rel, 1)
+    for j in range(depth):
+        await_block(8 * j + 6)
+        pass_on(8 * j + 6, 1)
+    for rel in range(1, count, 2):
+        await_block(rel)
+    for copy in mem_loads:
+        copy.wait()
+    mem_rows = mem_ref.reshape(members, lane_tiles, lons * var_count, LANES)
+    margin = HALF * var_count
+
+    def lat_step(d, carry):
+        at = pl.multiple_of(d * two, 16)
+        products = [
+            [
+                mem_rows[m, t, pl.ds(at, two), :] * whole_ref[d, :, tile_cols(t)]
+                for t in range(lane_tiles)
+            ]
+            for m in range(members)
+        ]
+        sides = [
+            jnp.dot(
+                jnp.concatenate(
+                    [jnp.concatenate(p[side : side + 2], axis=1) for p in products], axis=0
+                ),
+                lat_ref[side],
+                preferred_element_type=jnp.float32,
+            )
+            for side in range(2)
+        ]
+        bands = [
+            sides[0][:, :LANES],
+            sides[0][:, LANES:] + sides[1][:, :LANES],
+            sides[1][:, LANES:],
+        ]
+        for t, band in enumerate(bands):
+            narrow = band.astype(jnp.bfloat16)
+            for m in range(members):
+                banded_ref[pl.ds(at + margin, two), tile_cols(t * members + m)] = narrow[
+                    m * two : (m + 1) * two
+                ]
+        return carry
+
+    lax.fori_loop(0, count, lat_step, 0)
+    high_rows = lons * var_count
+    banded_ref[:margin] = banded_ref[high_rows : high_rows + margin]
+    banded_ref[high_rows + margin :] = banded_ref[margin : 2 * margin]
+
+    band_rows, band_depth = lon_ref.shape
+
+    def lon_step(q, carry):
+        at = pl.multiple_of(q * band_rows, 16)
+        for t in range(lane_tiles):
+            total = jnp.zeros((band_rows, LANES), jnp.float32)
+            for m in range(0, members, 2):
+                start = (t * members + m) * LANES
+                spread = jnp.dot(
+                    lon_ref[...],
+                    banded_ref[pl.ds(at, band_depth), start : start + 2 * LANES],
+                    preferred_element_type=jnp.float32,
+                )
+                for k in range(2):
+                    total += (
+                        mem_rows[m + k, t, pl.ds(at, band_rows), :].astype(jnp.float32)
+                        * spread[:, tile_cols(k)]
+                    )
+            contrib_ref[pl.ds(at + 8, band_rows), tile_cols(t)] = total
+        return carry
+
+    lax.fori_loop(0, high_rows // band_rows, lon_step, 0)
+    contrib_ref[:8] = contrib_ref[high_rows : high_rows + 8]
+    contrib_ref[high_rows + 8 :] = contrib_ref[8:16]
+
+    for copy in sends:
+        copy.wait_send()
+
+    def part_of(rel):
+        at = pl.multiple_of(flip_all(me, rel) * two, 16)
+        body = contrib_ref[pl.ds(at + 8, two), :]
+        ahead = contrib_ref[pl.ds(at, 8), :]
+        behind = contrib_ref[pl.ds(at + 8 + two, 8), :]
+        row = lax.broadcasted_iota(jnp.int32, (8, lats), 0)
+        return body, jnp.where(row < 4, behind, ahead)
+
+    reduce_sends = []
+
+    def ship(value, slot, stride):
+        out_buf[slot, :two] = value[0].astype(jnp.bfloat16)
+        out_buf[slot, two:] = value[1].astype(jnp.bfloat16)
+        copy = pltpu.make_async_remote_copy(
+            src_ref=out_buf.at[slot],
+            dst_ref=in_buf.at[slot],
+            send_sem=r_send.at[slot],
+            recv_sem=r_recv.at[slot],
+            device_id={"space": flip_all(me, stride)},
+            device_id_type=pl.DeviceIdType.MESH,
+        )
+        copy.start()
+        reduce_sends.append(copy)
+        return copy
+
+    flying = {}
+
+    def arrived(value, slot):
+        flying[slot].wait_recv()
+        return (
+            value[0] + in_buf[slot, :two].astype(jnp.float32),
+            value[1] + in_buf[slot, two:].astype(jnp.float32),
+        )
+
+    pair_slot = {}
+    column_of = {6: 0, 2: 1, 4: 2, 0: 3}
+    far = list(range(depth))[::-1]
+    for column in (6, 2, 4, 0):
+        for j in far:
+            slot = column_of[column] * depth + j
+            flying[slot] = ship(part_of(8 * j + column + 1), slot, 1)
+
+    def chip_part(column, j):
+        return arrived(part_of(8 * j + column), column_of[column] * depth + j)
+
+    base = 4 * depth
+    for j in far:
+        slot = base + j
+        flying[slot] = ship(chip_part(6, j), slot, 2 if j in forks else 4)
+    for column in (2, 4):
+        for j in far:
+            if (column == 2) == (j in forks):
+                slot = base + column // 2 * depth + j
+                flying[slot] = ship(chip_part(column, j), slot, column)
+    for j in far:
+        column = 4 if j in forks else 2
+        slot = base + column // 2 * depth + j
+        value = arrived(chip_part(column, j), base + j)
+        flying[slot] = ship(value, slot, column)
+    last = base + 3 * depth
+    value = None
+    for j in far:
+        value = chip_part(0, j)
+        for column in (2, 4):
+            value = arrived(value, base + column // 2 * depth + j)
+        if j:
+            flying[last + j] = ship(value, last + j, 8 * j)
+    for j in range(1, depth):
+        value = arrived(value, last + j)
+    body = value[0] / (total_members - 1.0)
+    rim = value[1] / (total_members - 1.0)
+    stage_rows = stage_ref.reshape(2, lane_tiles, two, LANES)
+    for t in range(lane_tiles):
+        total_ref[t, 0:8, :] = rim[:, tile_cols(t)]
+        total_ref[t, 8 : 8 + two, :] = body[:, tile_cols(t)]
+        total_ref[t, 8 + two :, :] = rim[:, tile_cols(t)]
+        stage_rows[0, t] = body[:, tile_cols(t)]
+    stores = []
+
+    def store(index, target):
+        for t in range(lane_tiles):
+            copy = pltpu.make_async_copy(
+                stage_ref.at[index, t], target.at[:, :, tile_cols(t)], out_sem.at[index, t]
+            )
+            copy.start()
+            stores.append(copy)
+
+    store(0, incr_hbm)
+
+    wide = rows + 4
+    for c in range(var_count):
+        values = tile_rows(total_ref, pl.ds(4 + c, wide, stride=var_count))
+        for b in range(3):
+            moved = shifted(values, b)
+            for t in range(lane_tiles):
+                taps_ref[0, t, pl.ds(2 * b + c, wide, stride=8), :] = moved[:, tile_cols(t)]
+
+    def tail_pair(p, carry):
+        for chunk in lane_chunks():
+            lines = [(2 * p + line, t) for line, t in chunk]
+            field = jnp.concatenate([tap_block(0, j, t) for j, t in lines], axis=1)
+            tangent = jnp.dot(
+                w_tail[...], field.astype(jnp.bfloat16), preferred_element_type=jnp.float32
+            )
+            slopes = jnp.concatenate([slopes_ref[j, :, tile_cols(t)] for j, t in lines], axis=1)
+            pieces = jnp.dot(
+                v_tail[...],
+                (slopes * tangent).astype(jnp.bfloat16),
+                preferred_element_type=jnp.float32,
+            )
+            for place, (j, t) in enumerate(lines):
+                part_ref[j, :, tile_cols(t)] = pieces[:24, tile_cols(place)]
+        return carry
+
+    lax.fori_loop(0, pairs, tail_pair, 0)
+    gather_pieces()
+    for c in range(var_count):
+        values = tile_rows(total_ref, pl.ds(8 + c, rows, stride=var_count)) + assembled(c)
+        for t in range(lane_tiles):
+            stage_rows[1, t, pl.ds(c, rows, stride=var_count), :] = values[:, tile_cols(t)]
+    store(1, resp_hbm)
+    for copy in stores:
+        copy.wait()
+    for copy in reduce_sends:
+        copy.wait_send()
+
+
+def whole_step(members, state, cotangent, conv_in, conv_out, bias):
+    count = lax.axis_size("space")
+    mine, lons, var_count, lats = members.shape
+    rows = state.shape[0]
+    hidden = bias.shape[0]
+    two = rows * var_count
+    tiles = lats // LANES
+    depth = count // 8
+    any_space = pl.BlockSpec(memory_space=pl.ANY)
+    vmem = pltpu.VMEM
+    dma = pltpu.SemaphoreType.DMA
+    margin = HALF * var_count
+    window = lats - LANES
+    slots = 8 * depth
+    return pl.pallas_call(
+        functools.partial(step_kernel, count, mine * count),
+        out_shape=(jax.ShapeDtypeStruct(state.shape, jnp.float32),) * 2,
+        in_specs=[any_space] * 6,
+        out_specs=(any_space,) * 2,
+        scratch_shapes=[
+            vmem((mine, tiles, lons, var_count, LANES), jnp.bfloat16),
+            vmem((2, tiles, rows, var_count, LANES), jnp.float32),
+            vmem((2, 2, tiles, 2, var_count, LANES), jnp.float32),
+            vmem((2, tiles, (rows + 5) * 8, LANES), jnp.float32),
+            vmem((2, 3, 3, var_count, hidden), jnp.float32),
+            vmem((1, hidden), jnp.float32),
+            vmem((4, 32, hidden), jnp.float32),
+            vmem((hidden, 96), jnp.bfloat16),
+            vmem((hidden, 96), jnp.bfloat16),
+            vmem((64, 2 * hidden), jnp.bfloat16),
+            vmem((hidden, 32), jnp.bfloat16),
+            vmem((32, hidden), jnp.bfloat16),
+            vmem((rows + 2, hidden, lats), jnp.float32),
+            vmem((rows + 2, 24, lats), jnp.float32),
+            vmem((tiles, rows * 8, LANES), jnp.float32),
+            vmem((tiles, two, LANES), jnp.float32),
+            vmem((count, two, lats), jnp.bfloat16),
+            vmem((2, window, window), jnp.bfloat16),
+            vmem((4 * two, 4 * two + 2 * margin), jnp.bfloat16),
+            vmem((lons * var_count + 2 * margin, mine * lats), jnp.bfloat16),
+            vmem((lons * var_count + 16, lats), jnp.float32),
+            vmem((slots, two + 8, lats), jnp.bfloat16),
+            vmem((slots, two + 8, lats), jnp.bfloat16),
+            vmem((tiles, two + 16, LANES), jnp.float32),
+            vmem((2, tiles, rows, var_count, LANES), jnp.float32),
+            dma((mine, tiles)),
+            dma((2, tiles)),
+            dma((3,)),
+            dma((2,)),
+            dma((2,)),
+            dma((count,)),
+            dma((count,)),
+            dma((slots,)),
+            dma((slots,)),
+            dma((2, tiles)),
+        ],
+        compiler_params=pltpu.CompilerParams(collective_id=2, has_side_effects=True),
+        name="whole_step",
+    )(
+        members,
+        state,
+        cotangent,
+        jnp.transpose(conv_in, (0, 1, 3, 2)),
+        conv_out,
+        bias.reshape(1, hidden),
+    )
+
+
+def fits(members, state, bias):
+    count = lax.axis_size("space")
+    mine, lons, var_count, lats = members.shape
+    rows = state.shape[0]
+    return (
+        lax.axis_size("mem") == 1
+        and count >= 8
+        and count & (count - 1) == 0
+        and var_count == 2
+        and lats == 3 * LANES
+        and rows % 8 == 0
+        and rows >= 2 * 8
+        and mine % 2 == 0
+        and lons == count * rows
+        and bias.shape[0] == LANES
+    )
+
+
 def per_device(members, state, cotangent, conv_in, conv_out, bias):
     row_count, var_count, lat_count = state.shape
+    if fits(members, state, bias):
+        return whole_step(members, state, cotangent, conv_in, conv_out, bias)
     count = lax.axis_size("space")
     direct = count >= 8 and count & (count - 1) == 0
     rim_width = 2

time: 105 us -> 68.7 us (0.65)
  matrix products: 15.6 us -> 0 us
  local copies, waits for them, and re-layouts: 17 us -> 3.07 us
  Pallas kernels: 55.6 us -> 64.7 us
  other arithmetic: 8.45 us -> 0 us
  starting transfers between devices: 6.52 us -> 0 us
    dot_general x4 -> x0, matrix products: 15.6 us -> none  [the longest x2 10.5 us: convolve(): jnp.einsum('ok,xky->xoy', flattened, stacked, precision=precision, prefer...]
    reshape x6 -> x0, local copies, waits for them, and re-layouts: 12.2 us -> none  [the longest x1 11.4 us: per_device(): merged = members.reshape(members.shape[0], members.shape[1], width)]
    pallas_call x3 -> x1, Pallas kernels: 55.6 us -> 64.7 us  [whole_step(): pl.pallas_call(functools.partial(step_kernel, count, mine * count), out_s...]
    ppermute x2 -> x0, starting transfers between devices: 6.52 us -> none  [the longest x1 5.97 us: padded_2(): lax.ppermute(head, axis, [((i + 1) % count, i) for i in range(count)])]
    convert_element_type x6 -> x0, other arithmetic: 5.1 us -> none  [the longest x2 2.62 us: band_matrix(): jnp.where(distance <= HALF, 1.0 - ratio * ratio, 0.0).astype(jnp.bfloat16)]
    unnamed x9 -> x2, local copies, waits for them, and re-layouts: 0.65 us -> 3.07 us
    concatenate x3 -> x0, local copies, waits for them, and re-layouts: 2.32 us -> none  [convolve(): jnp.concatenate([lat_padded[step_lon:step_lon + row_count, :, step_lat:st...]
    slice x11 -> x0, local copies, waits for them, and re-layouts: 1.84 us -> none  [the longest x8 1.73 us: convolve(): lat_padded[step_lon:step_lon + row_count, :, step_lat:step_lat + lat_count]]
  transfers between devices with their start and end apart: 2 -> 0, of which waited for: 0 -> 0; matrix products, arithmetic and copies ran while one was open for 16% -> 0% of each run, Pallas kernels for 0% -> 0%
where the time goes in v1:
time: 68.7 us; the launch traced here: 68.4 us
  Pallas kernels  64.7 us (94%)
  local copies, waits for them, and re-layouts  3.07 us (4%)
    pallas_call x1, Pallas kernels, whole_step(): pl.pallas_call(functools.partial(step_kernel, count, mine * count), out_s...  64.7 us
    unnamed x2, local copies, waits for them, and re-layouts  3.07 us

profile of v1, /device:TPU:0, one launch (start us, length us, event | category | flops | bytes accessed | tf_op | source)
XLA Modules:
  0.0 68.4 jit_solution(9790068780202839322)
XLA Ops:
  0.6 64.7 %whole_step.1 = (f32[24,2,384]{2,1,0:T(2,128)}, f32[24,2,384]{2,1,0:T(2,128)}) custom-call(bf16[4,768,2,384]{3,2,1,0:T(2,128)(2,1)} %members_hbm.1, f32[24,2,384]{2,1,0:T(2,128)} %state_hbm.1, f32[24,2,384]{2,1,0:T(2,128)} %cot_hbm.1, f32[3,3,2,128]{3,2,1,0:T(2,128)} %bitcast.2, f32[3,3,2,128]{3,2,1,0:T(2,128)} %wout_hbm.1, f32[1,128]{1,0:T(1,128)} %bitcast.3), custom_call_target="tpu_custom_call" | custom-call | tf_op jit(solution)/shard_map/whole_step/pallas_call | solution.py:830
  65.4 1.5 %copy.10 = f32[24,2,384]{2,1,0:T(2,128)} copy(f32[24,2,384]{2,1,0:T(2,128)} %get-tuple-element.4) | data formatting | bytes 147456
  66.9 1.5 %copy.11 = f32[24,2,384]{2,1,0:T(2,128)} copy(f32[24,2,384]{2,1,0:T(2,128)} %get-tuple-element.5) | data formatting | bytes 147456

commit v2 on v1

--- a/solution.py
+++ b/solution.py
@@ -9,6 +9,9 @@
 
 HALF = 16
 LANES = 128
+HEAD_GROUP = 11
+TAIL_GROUP = 13
+LAT_GROUP = 8
 
 
 def flip(index, stride):
@@ -359,14 +362,15 @@
     incr_hbm, resp_hbm,
     mem_ref, own_ref, halo_ref, taps_ref, wraw_ref, bias_ref, slot_ref,
     w_state, w_cot, v_in, w_tail, v_tail,
-    slopes_ref, part_ref, q_ref, g_ref, whole_ref, lat_ref, lon_ref, banded_ref, contrib_ref,
+    slopes_ref, back_ref, part_ref, q_ref, g_ref, whole_ref, lat_ref, lon_ref, banded_ref, contrib_ref,
     out_buf, in_buf, total_ref, stage_ref,
     mem_sem, own_sem, small_sem, halo_send, halo_recv, g_send, g_recv, r_send, r_recv, out_sem,
 ):
     me = lax.axis_index("space")
-    members, lane_tiles, lons, var_count, _ = mem_ref.shape
-    rows = own_ref.shape[2]
-    two = rows * var_count
+    members, lane_tiles, high_rows, _ = mem_ref.shape
+    var_count = wraw_ref.shape[3]
+    two = own_ref.shape[2]
+    rows = two // var_count
     lats = lane_tiles * LANES
     hidden = slot_ref.shape[2]
     depth = count // 8
@@ -376,7 +380,9 @@
     for index, source in enumerate((state_hbm, cot_hbm)):
         for t in range(lane_tiles):
             copy = pltpu.make_async_copy(
-                source.at[:, :, tile_cols(t)], own_ref.at[index, t], own_sem.at[index, t]
+                source.reshape(two, lats).at[:, tile_cols(t)],
+                own_ref.at[index, t],
+                own_sem.at[index, t],
             )
             copy.start()
             own_loads.append(copy)
@@ -388,10 +394,11 @@
     for copy in small_loads:
         copy.start()
     mem_loads = []
+    flat_members = members_hbm.reshape(members, high_rows, lats)
     for m in range(members):
         for t in range(lane_tiles):
             copy = pltpu.make_async_copy(
-                members_hbm.at[m, :, :, tile_cols(t)], mem_ref.at[m, t], mem_sem.at[m, t]
+                flat_members.at[m, :, tile_cols(t)], mem_ref.at[m, t], mem_sem.at[m, t]
             )
             copy.start()
             mem_loads.append(copy)
@@ -447,9 +454,9 @@
         copy.wait()
     pl.semaphore_wait(barrier, len(friends))
     edges = []
-    for side, start, friend in ((1, 0, before), (0, rows - 2, after)):
+    for side, start, friend in ((1, 0, before), (0, two - 8, after)):
         copy = pltpu.make_async_remote_copy(
-            src_ref=own_ref.at[:, :, start : start + 2],
+            src_ref=own_ref.at[:, :, start : start + 8],
             dst_ref=halo_ref.at[side],
             send_sem=halo_send.at[side],
             recv_sem=halo_recv.at[side],
@@ -459,11 +466,10 @@
         copy.start()
         edges.append(copy)
 
-    own_rows = own_ref.reshape(2, lane_tiles, two, LANES)
     for index in range(2):
         for c in range(var_count):
             values = jnp.concatenate(
-                [own_rows[index, t, pl.ds(c, rows, stride=var_count), :] for t in range(lane_tiles)],
+                [own_ref[index, t, pl.ds(c, rows, stride=var_count), :] for t in range(lane_tiles)],
                 axis=1,
             )
             for b in range(3):
@@ -476,12 +482,23 @@
         return [tiles[k : k + 2] for k in range(0, len(tiles), 2)]
 
     def tap_block(index, j, t):
-        start = pl.multiple_of(8 * j, 8)
+        start = 8 * j if isinstance(j, int) else pl.multiple_of(8 * j, 8)
         return taps_ref[index, t, pl.ds(start, 32), :]
 
     def fine_block(index, j, t):
         high, low = halves(tap_block(index, j, t))
         return jnp.concatenate([high, low, high], axis=0)
+
+    def in_groups(step, first, last, group):
+        def several(k, carry):
+            for place in range(group):
+                step(first + k * group + place)
+            return carry
+
+        full = (last - first) // group
+        lax.fori_loop(0, full, several, 0)
+        for p in range(first + full * group, last):
+            step(p)
 
     def head_pair(p):
         for chunk in lane_chunks():
@@ -491,30 +508,37 @@
             activity = jnp.tanh(jnp.dot(w_state[...], field, preferred_element_type=jnp.float32))
             slopes = 1.0 - activity * activity
             back = slopes * jnp.dot(w_cot[...], misfit, preferred_element_type=jnp.float32)
-            high, low = halves(back)
-            pieces = jnp.dot(
-                v_in[...], jnp.concatenate([high, low], axis=0), preferred_element_type=jnp.float32
-            )
-            pieces = pieces[:24] + pieces[32:56]
+            back = jnp.concatenate(halves(back), axis=0)
             for place, (j, t) in enumerate(lines):
                 slopes_ref[j, :, tile_cols(t)] = slopes[:, tile_cols(place)]
-                part_ref[j, :, tile_cols(t)] = pieces[:, tile_cols(place)]
+                back_ref[j, :, tile_cols(t)] = back[:, tile_cols(place)]
+
+    def project_pair(weights, p):
+        for chunk in lane_chunks():
+            lines = [(2 * p + line, t) for line, t in chunk]
+            pieces = jnp.dot(
+                weights,
+                jnp.concatenate(
+                    [back_ref[j, : weights.shape[1], tile_cols(t)] for j, t in lines], axis=1
+                ),
+                preferred_element_type=jnp.float32,
+            )
+            if pieces.shape[0] > 32:
+                pieces = pieces[:32] + pieces[32:]
+            for place, (j, t) in enumerate(lines):
+                part_ref[j, :, tile_cols(t)] = pieces[:24, tile_cols(place)]
 
     pairs = (rows + 2) // 2
 
-    def inner(p, carry):
-        head_pair(p)
-        return carry
-
-    lax.fori_loop(1, pairs - 1, inner, 0)
+    in_groups(head_pair, 1, pairs - 1, HEAD_GROUP)
+    in_groups(functools.partial(project_pair, v_in[...]), 1, pairs - 1, HEAD_GROUP)
 
     for copy in edges:
         copy.wait()
-    halo_rows = halo_ref.reshape(2, 2, lane_tiles, 2 * var_count, LANES)
-    for side, slot in ((0, 0), (1, rows + 2)):
+    for side, slot, first in ((0, 0, 4), (1, rows + 2, 0)):
         for index in range(2):
             values = jnp.concatenate(
-                [halo_rows[side, index, t] for t in range(lane_tiles)], axis=1
+                [halo_ref[side, index, t] for t in range(lane_tiles)], axis=1
             )
             for b in range(3):
                 moved = shifted(values, b)
@@ -522,14 +546,13 @@
                     at = 8 * (slot + line) + 2 * b
                     for t in range(lane_tiles):
                         taps_ref[index, t, at : at + 2, :] = moved[
-                            2 * line : 2 * line + 2, tile_cols(t)
+                            first + 2 * line : first + 2 * line + 2, tile_cols(t)
                         ]
 
-    def outer(p, carry):
-        head_pair(p * (pairs - 1))
-        return carry
-
-    lax.fori_loop(0, 2, outer, 0)
+    for p in (0, pairs - 1):
+        head_pair(p)
+    for p in (0, pairs - 1):
+        project_pair(v_in[...], p)
 
     def assembled(c):
         return sum(
@@ -552,7 +575,7 @@
     gather_pieces()
     for c in range(var_count):
         values = jnp.concatenate(
-            [own_rows[1, t, pl.ds(c, rows, stride=var_count), :] for t in range(lane_tiles)], axis=1
+            [own_ref[1, t, pl.ds(c, rows, stride=var_count), :] for t in range(lane_tiles)], axis=1
         )
         values = values + assembled(c)
         for t in range(lane_tiles):
@@ -618,16 +641,18 @@
         await_block(rel)
     for copy in mem_loads:
         copy.wait()
-    mem_rows = mem_ref.reshape(members, lane_tiles, lons * var_count, LANES)
     margin = HALF * var_count
 
+    span = LAT_GROUP * two
+
     def lat_step(d, carry):
-        at = pl.multiple_of(d * two, 16)
+        at = pl.multiple_of(d * span, 16)
+        fields = [
+            whole_ref[pl.ds(d * LAT_GROUP, LAT_GROUP), :, tile_cols(t)].reshape(span, LANES)
+            for t in range(lane_tiles)
+        ]
         products = [
-            [
-                mem_rows[m, t, pl.ds(at, two), :] * whole_ref[d, :, tile_cols(t)]
-                for t in range(lane_tiles)
-            ]
+            [mem_ref[m, t, pl.ds(at, span), :] * fields[t] for t in range(lane_tiles)]
             for m in range(members)
         ]
         sides = [
@@ -648,13 +673,12 @@
         for t, band in enumerate(bands):
             narrow = band.astype(jnp.bfloat16)
             for m in range(members):
-                banded_ref[pl.ds(at + margin, two), tile_cols(t * members + m)] = narrow[
-                    m * two : (m + 1) * two
+                banded_ref[pl.ds(at + margin, span), tile_cols(t * members + m)] = narrow[
+                    m * span : (m + 1) * span
                 ]
         return carry
 
-    lax.fori_loop(0, count, lat_step, 0)
-    high_rows = lons * var_count
+    lax.fori_loop(0, count // LAT_GROUP, lat_step, 0)
     banded_ref[:margin] = banded_ref[high_rows : high_rows + margin]
     banded_ref[high_rows + margin :] = banded_ref[margin : 2 * margin]
 
@@ -673,7 +697,7 @@
                 )
                 for k in range(2):
                     total += (
-                        mem_rows[m + k, t, pl.ds(at, band_rows), :].astype(jnp.float32)
+                        mem_ref[m + k, t, pl.ds(at, band_rows), :].astype(jnp.float32)
                         * spread[:, tile_cols(k)]
                     )
             contrib_ref[pl.ds(at + 8, band_rows), tile_cols(t)] = total
@@ -757,18 +781,19 @@
         value = arrived(value, last + j)
     body = value[0] / (total_members - 1.0)
     rim = value[1] / (total_members - 1.0)
-    stage_rows = stage_ref.reshape(2, lane_tiles, two, LANES)
     for t in range(lane_tiles):
         total_ref[t, 0:8, :] = rim[:, tile_cols(t)]
         total_ref[t, 8 : 8 + two, :] = body[:, tile_cols(t)]
         total_ref[t, 8 + two :, :] = rim[:, tile_cols(t)]
-        stage_rows[0, t] = body[:, tile_cols(t)]
+        stage_ref[0, t] = body[:, tile_cols(t)]
     stores = []
 
     def store(index, target):
         for t in range(lane_tiles):
             copy = pltpu.make_async_copy(
-                stage_ref.at[index, t], target.at[:, :, tile_cols(t)], out_sem.at[index, t]
+                stage_ref.at[index, t],
+                target.reshape(two, lats).at[:, tile_cols(t)],
+                out_sem.at[index, t],
             )
             copy.start()
             stores.append(copy)
@@ -783,7 +808,7 @@
             for t in range(lane_tiles):
                 taps_ref[0, t, pl.ds(2 * b + c, wide, stride=8), :] = moved[:, tile_cols(t)]
 
-    def tail_pair(p, carry):
+    def tail_pair(p):
         for chunk in lane_chunks():
             lines = [(2 * p + line, t) for line, t in chunk]
             field = jnp.concatenate([tap_block(0, j, t) for j, t in lines], axis=1)
@@ -791,21 +816,17 @@
                 w_tail[...], field.astype(jnp.bfloat16), preferred_element_type=jnp.float32
             )
             slopes = jnp.concatenate([slopes_ref[j, :, tile_cols(t)] for j, t in lines], axis=1)
-            pieces = jnp.dot(
-                v_tail[...],
-                (slopes * tangent).astype(jnp.bfloat16),
-                preferred_element_type=jnp.float32,
-            )
+            back = (slopes * tangent).astype(jnp.bfloat16)
             for place, (j, t) in enumerate(lines):
-                part_ref[j, :, tile_cols(t)] = pieces[:24, tile_cols(place)]
-        return carry
-
-    lax.fori_loop(0, pairs, tail_pair, 0)
+                back_ref[j, :hidden, tile_cols(t)] = back[:, tile_cols(place)]
+
+    in_groups(tail_pair, 0, pairs, TAIL_GROUP)
+    in_groups(functools.partial(project_pair, v_tail[...]), 0, pairs, TAIL_GROUP)
     gather_pieces()
     for c in range(var_count):
         values = tile_rows(total_ref, pl.ds(8 + c, rows, stride=var_count)) + assembled(c)
         for t in range(lane_tiles):
-            stage_rows[1, t, pl.ds(c, rows, stride=var_count), :] = values[:, tile_cols(t)]
+            stage_ref[1, t, pl.ds(c, rows, stride=var_count), :] = values[:, tile_cols(t)]
     store(1, resp_hbm)
     for copy in stores:
         copy.wait()
@@ -833,9 +854,9 @@
         in_specs=[any_space] * 6,
         out_specs=(any_space,) * 2,
         scratch_shapes=[
-            vmem((mine, tiles, lons, var_count, LANES), jnp.bfloat16),
-            vmem((2, tiles, rows, var_count, LANES), jnp.float32),
-            vmem((2, 2, tiles, 2, var_count, LANES), jnp.float32),
+            vmem((mine, tiles, lons * var_count, LANES), jnp.bfloat16),
+            vmem((2, tiles, two, LANES), jnp.float32),
+            vmem((2, 2, tiles, 8, LANES), jnp.float32),
             vmem((2, tiles, (rows + 5) * 8, LANES), jnp.float32),
             vmem((2, 3, 3, var_count, hidden), jnp.float32),
             vmem((1, hidden), jnp.float32),
@@ -846,6 +867,7 @@
             vmem((hidden, 32), jnp.bfloat16),
             vmem((32, hidden), jnp.bfloat16),
             vmem((rows + 2, hidden, lats), jnp.float32),
+            vmem((rows + 2, 2 * hidden, lats), jnp.bfloat16),
             vmem((rows + 2, 24, lats), jnp.float32),
             vmem((tiles, rows * 8, LANES), jnp.float32),
             vmem((tiles, two, LANES), jnp.float32),
@@ -857,7 +879,7 @@
             vmem((slots, two + 8, lats), jnp.bfloat16),
             vmem((slots, two + 8, lats), jnp.bfloat16),
             vmem((tiles, two + 16, LANES), jnp.float32),
-            vmem((2, tiles, rows, var_count, LANES), jnp.float32),
+            vmem((2, tiles, two, LANES), jnp.float32),
             dma((mine, tiles)),
             dma((2, tiles)),
             dma((3,)),

time: 68.7 us -> 47.2 us (0.69)
  Pallas kernels: 64.7 us -> 43.3 us
    pallas_call x1, Pallas kernels: 64.7 us -> 43.3 us  [whole_step(): pl.pallas_call(functools.partial(step_kernel, count, mine * count), out_s...]
where the time goes in v2:
time: 47.2 us; the launch traced here: 47 us
  Pallas kernels  43.3 us (92%)
  local copies, waits for them, and re-layouts  3.07 us (7%)
  between operations  0.64 us (1%)
    pallas_call x1, Pallas kernels, whole_step(): pl.pallas_call(functools.partial(step_kernel, count, mine * count), out_s...  43.3 us
    unnamed x2, local copies, waits for them, and re-layouts  3.07 us

profile of v2, /device:TPU:0, one launch (start us, length us, event | category | flops | bytes accessed | tf_op | source)
XLA Modules:
  0.0 47.0 jit_solution(6397662967782544196)
XLA Ops:
  0.6 43.3 %whole_step.1 = (f32[24,2,384]{2,1,0:T(2,128)}, f32[24,2,384]{2,1,0:T(2,128)}) custom-call(bf16[4,768,2,384]{3,2,1,0:T(2,128)(2,1)} %members_hbm.1, f32[24,2,384]{2,1,0:T(2,128)} %state_hbm.1, f32[24,2,384]{2,1,0:T(2,128)} %cot_hbm.1, f32[3,3,2,128]{3,2,1,0:T(2,128)} %bitcast.2, f32[3,3,2,128]{3,2,1,0:T(2,128)} %wout_hbm.1, f32[1,128]{1,0:T(1,128)} %bitcast.3), custom_call_target="tpu_custom_call" | custom-call | tf_op jit(solution)/shard_map/whole_step/pallas_call | solution.py:851
  43.9 1.5 %copy.10 = f32[24,2,384]{2,1,0:T(2,128)} copy(f32[24,2,384]{2,1,0:T(2,128)} %get-tuple-element.4) | data formatting | bytes 147456
  45.4 1.5 %copy.11 = f32[24,2,384]{2,1,0:T(2,128)} copy(f32[24,2,384]{2,1,0:T(2,128)} %get-tuple-element.5) | data formatting | bytes 147456

commit v3 on v2

--- a/solution.py
+++ b/solution.py
@@ -11,7 +11,6 @@
 LANES = 128
 HEAD_GROUP = 11
 TAIL_GROUP = 13
-LAT_GROUP = 8
 
 
 def flip(index, stride):
@@ -359,12 +358,12 @@
 def step_kernel(
     count, total_members,
     members_hbm, state_hbm, cot_hbm, win_hbm, wout_hbm, bias_hbm,
-    incr_hbm, resp_hbm,
+    stage_ref,
     mem_ref, own_ref, halo_ref, taps_ref, wraw_ref, bias_ref, slot_ref,
     w_state, w_cot, v_in, w_tail, v_tail,
-    slopes_ref, back_ref, part_ref, q_ref, g_ref, whole_ref, lat_ref, lon_ref, banded_ref, contrib_ref,
-    out_buf, in_buf, total_ref, stage_ref,
-    mem_sem, own_sem, small_sem, halo_send, halo_recv, g_send, g_recv, r_send, r_recv, out_sem,
+    slopes_ref, back_ref, part_ref, q_ref, g_ref, whole_ref, lat_ref, lon_ref, rim_ref, banded_ref, contrib_ref,
+    out_buf, in_buf, total_ref,
+    mem_sem, own_sem, small_sem, halo_send, halo_recv, g_send, g_recv, r_send, r_recv,
 ):
     me = lax.axis_index("space")
     members, lane_tiles, high_rows, _ = mem_ref.shape
@@ -429,6 +428,11 @@
     gap = i - j + var_count * HALF
     value = tap_of(jnp.abs(gap).astype(jnp.float32) * 0.5)
     lon_ref[...] = jnp.where((gap & 1) == 0, value, 0.0).astype(jnp.bfloat16)
+    i = lax.broadcasted_iota(jnp.int32, rim_ref.shape, 0)
+    j = lax.broadcasted_iota(jnp.int32, rim_ref.shape, 1)
+    gap = i - j + rim_ref.shape[1] // 2 - 8
+    value = tap_of(jnp.abs(gap).astype(jnp.float32) * 0.5)
+    rim_ref[...] = jnp.where((gap & 1) == 0, value, 0.0).astype(jnp.bfloat16)
 
     for copy in small_loads:
         copy.wait()
@@ -627,28 +631,14 @@
                 if (near == 4) == (j in forks):
                     pass_on(near, 6 - near)
                 pass_on(near, 1)
-    for j in range(1, depth):
-        for near in (2, 4):
-            rel = 8 * j + near
-            await_block(rel)
-            if (near == 4) == (j in forks):
-                pass_on(rel, 6 - near)
-            pass_on(rel, 1)
-    for j in range(depth):
-        await_block(8 * j + 6)
-        pass_on(8 * j + 6, 1)
-    for rel in range(1, count, 2):
-        await_block(rel)
-    for copy in mem_loads:
-        copy.wait()
-    margin = HALF * var_count
-
-    span = LAT_GROUP * two
-
-    def lat_step(d, carry):
+    margin = (banded_ref.shape[0] - high_rows) // 2
+    group = count // depth
+    span = group * two
+
+    def lat_step(d):
         at = pl.multiple_of(d * span, 16)
         fields = [
-            whole_ref[pl.ds(d * LAT_GROUP, LAT_GROUP), :, tile_cols(t)].reshape(span, LANES)
+            whole_ref[pl.ds(d * group, group), :, tile_cols(t)].reshape(span, LANES)
             for t in range(lane_tiles)
         ]
         products = [
@@ -676,13 +666,40 @@
                 banded_ref[pl.ds(at + margin, span), tile_cols(t * members + m)] = narrow[
                     m * span : (m + 1) * span
                 ]
-        return carry
-
-    lax.fori_loop(0, count // LAT_GROUP, lat_step, 0)
+
+    def near_blocks(j):
+        for near in (2, 4):
+            rel = 8 * j + near
+            await_block(rel)
+            if (near == 4) == (j in forks):
+                pass_on(rel, 6 - near)
+            pass_on(rel, 1)
+
+    for copy in mem_loads:
+        copy.wait()
+    def finish(j):
+        await_block(8 * j + 6)
+        pass_on(8 * j + 6, 1)
+
+    def band(j):
+        for column in range(1, 8, 2):
+            await_block(8 * j + column)
+        lat_step(flip_all(me, 8 * j) // 8)
+
+    lead = min(1, depth - 1)
+    for j in range(1, depth):
+        near_blocks(j)
+    for j in range(depth + lead):
+        if j < depth:
+            finish(j)
+        if j >= lead:
+            band(j - lead)
+
     banded_ref[:margin] = banded_ref[high_rows : high_rows + margin]
     banded_ref[high_rows + margin :] = banded_ref[margin : 2 * margin]
 
     band_rows, band_depth = lon_ref.shape
+    inset = margin - (band_depth - band_rows) // 2
 
     def lon_step(q, carry):
         at = pl.multiple_of(q * band_rows, 16)
@@ -692,7 +709,7 @@
                 start = (t * members + m) * LANES
                 spread = jnp.dot(
                     lon_ref[...],
-                    banded_ref[pl.ds(at, band_depth), start : start + 2 * LANES],
+                    banded_ref[pl.ds(at + inset, band_depth), start : start + 2 * LANES],
                     preferred_element_type=jnp.float32,
                 )
                 for k in range(2):
@@ -703,9 +720,34 @@
             contrib_ref[pl.ds(at + 8, band_rows), tile_cols(t)] = total
         return carry
 
-    lax.fori_loop(0, high_rows // band_rows, lon_step, 0)
-    contrib_ref[:8] = contrib_ref[high_rows : high_rows + 8]
-    contrib_ref[high_rows + 8 :] = contrib_ref[8:16]
+    def lon_plane(p):
+        per = span // band_rows
+        lax.fori_loop(p * per, (p + 1) * per, lon_step, 0)
+
+    for p in range(depth):
+        at = p * span
+        ahead = (at - 8) % high_rows
+        for t in range(lane_tiles):
+            total = jnp.zeros((16, LANES), jnp.float32)
+            for m in range(0, members, 2):
+                start = (t * members + m) * LANES
+                spread = jnp.dot(
+                    rim_ref[...],
+                    banded_ref[at : at + 2 * margin, start : start + 2 * LANES],
+                    preferred_element_type=jnp.float32,
+                )
+                for k in range(2):
+                    near = jnp.concatenate(
+                        [
+                            mem_ref[m + k, t, ahead : ahead + 8, :].astype(jnp.float32),
+                            mem_ref[m + k, t, at : at + 8, :].astype(jnp.float32),
+                        ],
+                        axis=0,
+                    )
+                    total += near * spread[:, tile_cols(k)]
+            contrib_ref[at : at + 16, tile_cols(t)] = total
+            if p == 0:
+                contrib_ref[high_rows + 8 :, tile_cols(t)] = total[8:]
 
     for copy in sends:
         copy.wait_send()
@@ -744,39 +786,46 @@
             value[1] + in_buf[slot, two:].astype(jnp.float32),
         )
 
-    pair_slot = {}
     column_of = {6: 0, 2: 1, 4: 2, 0: 3}
     far = list(range(depth))[::-1]
-    for column in (6, 2, 4, 0):
-        for j in far:
+    base = 4 * depth
+    last = base + 3 * depth
+
+    def to_partner(j):
+        lon_plane(flip_all(me, 8 * j) // 8)
+        for column in (6, 2, 4, 0):
             slot = column_of[column] * depth + j
             flying[slot] = ship(part_of(8 * j + column + 1), slot, 1)
 
     def chip_part(column, j):
         return arrived(part_of(8 * j + column), column_of[column] * depth + j)
 
-    base = 4 * depth
-    for j in far:
-        slot = base + j
-        flying[slot] = ship(chip_part(6, j), slot, 2 if j in forks else 4)
-    for column in (2, 4):
-        for j in far:
-            if (column == 2) == (j in forks):
-                slot = base + column // 2 * depth + j
-                flying[slot] = ship(chip_part(column, j), slot, column)
-    for j in far:
-        column = 4 if j in forks else 2
-        slot = base + column // 2 * depth + j
-        value = arrived(chip_part(column, j), base + j)
-        flying[slot] = ship(value, slot, column)
-    last = base + 3 * depth
-    value = None
-    for j in far:
+    def to_sides(j):
+        first = 2 if j in forks else 4
+        flying[base + j] = ship(chip_part(6, j), base + j, first)
+        slot = base + first // 2 * depth + j
+        flying[slot] = ship(chip_part(first, j), slot, first)
+
+    def relayed(j):
+        second = 4 if j in forks else 2
+        slot = base + second // 2 * depth + j
+        flying[slot] = ship(arrived(chip_part(second, j), base + j), slot, second)
+
+    def column_sum(j):
         value = chip_part(0, j)
         for column in (2, 4):
             value = arrived(value, base + column // 2 * depth + j)
+        return value
+
+    def along(j):
         if j:
-            flying[last + j] = ship(value, last + j, 8 * j)
+            flying[last + j] = ship(column_sum(j), last + j, 8 * j)
+
+    for step in range(depth + 3):
+        for lag, action in enumerate((to_partner, to_sides, relayed, along)):
+            if 0 <= step - lag < depth:
+                action(far[step - lag])
+    value = column_sum(0)
     for j in range(1, depth):
         value = arrived(value, last + j)
     body = value[0] / (total_members - 1.0)
@@ -786,20 +835,6 @@
         total_ref[t, 8 : 8 + two, :] = body[:, tile_cols(t)]
         total_ref[t, 8 + two :, :] = rim[:, tile_cols(t)]
         stage_ref[0, t] = body[:, tile_cols(t)]
-    stores = []
-
-    def store(index, target):
-        for t in range(lane_tiles):
-            copy = pltpu.make_async_copy(
-                stage_ref.at[index, t],
-                target.reshape(two, lats).at[:, tile_cols(t)],
-                out_sem.at[index, t],
-            )
-            copy.start()
-            stores.append(copy)
-
-    store(0, incr_hbm)
-
     wide = rows + 4
     for c in range(var_count):
         values = tile_rows(total_ref, pl.ds(4 + c, wide, stride=var_count))
@@ -827,11 +862,24 @@
         values = tile_rows(total_ref, pl.ds(8 + c, rows, stride=var_count)) + assembled(c)
         for t in range(lane_tiles):
             stage_ref[1, t, pl.ds(c, rows, stride=var_count), :] = values[:, tile_cols(t)]
-    store(1, resp_hbm)
+    for copy in reduce_sends:
+        copy.wait_send()
+
+
+def emit_kernel(tiled_ref, incr_hbm, resp_hbm, out_sem):
+    _, tiles, two, _ = tiled_ref.shape
+    stores = []
+    for index, target in enumerate((incr_hbm, resp_hbm)):
+        for t in range(tiles):
+            copy = pltpu.make_async_copy(
+                tiled_ref.at[index, t],
+                target.reshape(two, tiles * LANES).at[:, tile_cols(t)],
+                out_sem.at[index, t],
+            )
+            copy.start()
+            stores.append(copy)
     for copy in stores:
         copy.wait()
-    for copy in reduce_sends:
-        copy.wait_send()
 
 
 def whole_step(members, state, cotangent, conv_in, conv_out, bias):
@@ -848,11 +896,11 @@
     margin = HALF * var_count
     window = lats - LANES
     slots = 8 * depth
-    return pl.pallas_call(
+    tiled = pl.pallas_call(
         functools.partial(step_kernel, count, mine * count),
-        out_shape=(jax.ShapeDtypeStruct(state.shape, jnp.float32),) * 2,
+        out_shape=jax.ShapeDtypeStruct((2, tiles, two, LANES), jnp.float32),
         in_specs=[any_space] * 6,
-        out_specs=(any_space,) * 2,
+        out_specs=pl.BlockSpec(memory_space=vmem),
         scratch_shapes=[
             vmem((mine, tiles, lons * var_count, LANES), jnp.bfloat16),
             vmem((2, tiles, two, LANES), jnp.float32),
@@ -874,12 +922,12 @@
             vmem((count, two, lats), jnp.bfloat16),
             vmem((2, window, window), jnp.bfloat16),
             vmem((4 * two, 4 * two + 2 * margin), jnp.bfloat16),
-            vmem((lons * var_count + 2 * margin, mine * lats), jnp.bfloat16),
+            vmem((16, 2 * (margin + 16)), jnp.bfloat16),
+            vmem((lons * var_count + 2 * (margin + 16), mine * lats), jnp.bfloat16),
             vmem((lons * var_count + 16, lats), jnp.float32),
             vmem((slots, two + 8, lats), jnp.bfloat16),
             vmem((slots, two + 8, lats), jnp.bfloat16),
             vmem((tiles, two + 16, LANES), jnp.float32),
-            vmem((2, tiles, two, LANES), jnp.float32),
             dma((mine, tiles)),
             dma((2, tiles)),
             dma((3,)),
@@ -889,7 +937,6 @@
             dma((count,)),
             dma((slots,)),
             dma((slots,)),
-            dma((2, tiles)),
         ],
         compiler_params=pltpu.CompilerParams(collective_id=2, has_side_effects=True),
         name="whole_step",
@@ -901,6 +948,14 @@
         conv_out,
         bias.reshape(1, hidden),
     )
+    return pl.pallas_call(
+        emit_kernel,
+        out_shape=(jax.ShapeDtypeStruct(state.shape, jnp.float32),) * 2,
+        in_specs=[pl.BlockSpec(memory_space=vmem)],
+        out_specs=(any_space,) * 2,
+        scratch_shapes=[dma((2, tiles))],
+        name="emit",
+    )(tiled)
 
 
 def fits(members, state, bias):

time: 47.2 us -> 43.9 us (0.930)
  local copies, waits for them, and re-layouts: 3.07 us -> 0 us
    unnamed x2 -> x0, local copies, waits for them, and re-layouts: 3.07 us -> none
    pallas_call x1, Pallas kernels: 43.3 us -> 41.5 us  [whole_step(): pl.pallas_call(functools.partial(step_kernel, count, mine * count), out_s...]
    pallas_call x0 -> x1, Pallas kernels: none -> 1.61 us  [whole_step(): pl.pallas_call(emit_kernel, out_shape=(jax.ShapeDtypeStruct(state.shape,...]
where the time goes in v3:
time: 43.9 us; the launch traced here: 43.8 us
  Pallas kernels  43.2 us (98%)
  between operations  0.64 us (1%)
    pallas_call x1, Pallas kernels, whole_step(): pl.pallas_call(functools.partial(step_kernel, count, mine * count), out_s...  41.5 us
    pallas_call x1, Pallas kernels, whole_step(): pl.pallas_call(emit_kernel, out_shape=(jax.ShapeDtypeStruct(state.shape,...  1.61 us

profile of v3, /device:TPU:0, one launch (start us, length us, event | category | flops | bytes accessed | tf_op | source)
XLA Modules:
  0.0 43.8 jit_solution(12918535539954462909)
XLA Ops:
  0.6 41.5 %whole_step.1.tiled_ref = f32[2,3,48,128]{3,2,1,0:T(8,128)} custom-call(bf16[4,768,2,384]{3,2,1,0:T(2,128)(2,1)} %members_hbm.1, f32[24,2,384]{2,1,0:T(2,128)} %state_hbm.1, f32[24,2,384]{2,1,0:T(2,128)} %cot_hbm.1, f32[3,3,2,128]{3,2,1,0:T(2,128)} %bitcast.2, f32[3,3,2,128]{3,2,1,0:T(2,128)} %wout_hbm.1, f32[1,128]{1,0:T(1,128)} %bitcast.3), custom_call_target="tpu_custom_call" | custom-call | tf_op jit(solution)/shard_map/whole_step/pallas_call | solution.py:899
  42.2 1.6 %emit.1 = (f32[24,2,384]{2,1,0:T(2,128)}, f32[24,2,384]{2,1,0:T(2,128)}) custom-call(f32[2,3,48,128]{3,2,1,0:T(8,128)} %whole_step.1.tiled_ref), custom_call_target="tpu_custom_call" | custom-call | tf_op jit(solution)/shard_map/emit/pallas_call | solution.py:951

commit v4 on v3

--- a/solution.py
+++ b/solution.py
@@ -403,7 +403,7 @@
             mem_loads.append(copy)
 
     barrier = pltpu.get_barrier_semaphore()
-    friends = [before, after] + [flip(me, 1), flip(me, 2), flip(me, 4)]
+    friends = [before, after, flip(me, 1), flip(me, 2), flip(me, 4), flip_all(me, 6)]
     friends += [flip_all(me, 8 * j) for j in range(1, depth)]
     for friend in friends:
         pl.semaphore_signal(
@@ -801,30 +801,26 @@
         return arrived(part_of(8 * j + column), column_of[column] * depth + j)
 
     def to_sides(j):
-        first = 2 if j in forks else 4
-        flying[base + j] = ship(chip_part(6, j), base + j, first)
-        slot = base + first // 2 * depth + j
-        flying[slot] = ship(chip_part(first, j), slot, first)
-
-    def relayed(j):
-        second = 4 if j in forks else 2
-        slot = base + second // 2 * depth + j
-        flying[slot] = ship(arrived(chip_part(second, j), base + j), slot, second)
+        for column, slot in ((6, base), (2, base + depth), (4, base + 2 * depth)):
+            flying[slot + j] = ship(chip_part(column, j), slot + j, column)
 
     def column_sum(j):
         value = chip_part(0, j)
-        for column in (2, 4):
-            value = arrived(value, base + column // 2 * depth + j)
+        for side in range(3):
+            value = arrived(value, base + side * depth + j)
         return value
 
     def along(j):
         if j:
             flying[last + j] = ship(column_sum(j), last + j, 8 * j)
 
-    for step in range(depth + 3):
-        for lag, action in enumerate((to_partner, to_sides, relayed, along)):
-            if 0 <= step - lag < depth:
-                action(far[step - lag])
+    for place, j in enumerate(far):
+        to_partner(j)
+        if place:
+            to_sides(far[place - 1])
+    to_sides(0)
+    for j in far:
+        along(j)
     value = column_sum(0)
     for j in range(1, depth):
         value = arrived(value, last + j)

time: 43.9 us -> 41.2 us (0.938)
  Pallas kernels: 43.2 us -> 40.4 us
    pallas_call x1, Pallas kernels: 41.5 us -> 38.8 us  [whole_step(): pl.pallas_call(functools.partial(step_kernel, count, mine * count), out_s...]
where the time goes in v4:
time: 41.2 us; the launch traced here: 41 us
  Pallas kernels  40.4 us (98%)
  between operations  0.64 us (2%)
    pallas_call x1, Pallas kernels, whole_step(): pl.pallas_call(functools.partial(step_kernel, count, mine * count), out_s...  38.8 us
    pallas_call x1, Pallas kernels, whole_step(): pl.pallas_call(emit_kernel, out_shape=(jax.ShapeDtypeStruct(state.shape,...  1.61 us

profile of v4, /device:TPU:0, one launch (start us, length us, event | category | flops | bytes accessed | tf_op | source)
XLA Modules:
  0.0 41.0 jit_solution(16567758713196786415)
XLA Ops:
  0.6 38.8 %whole_step.1.tiled_ref = f32[2,3,48,128]{3,2,1,0:T(8,128)} custom-call(bf16[4,768,2,384]{3,2,1,0:T(2,128)(2,1)} %members_hbm.1, f32[24,2,384]{2,1,0:T(2,128)} %state_hbm.1, f32[24,2,384]{2,1,0:T(2,128)} %cot_hbm.1, f32[3,3,2,128]{3,2,1,0:T(2,128)} %bitcast.2, f32[3,3,2,128]{3,2,1,0:T(2,128)} %wout_hbm.1, f32[1,128]{1,0:T(1,128)} %bitcast.3), custom_call_target="tpu_custom_call" | custom-call | tf_op jit(solution)/shard_map/whole_step/pallas_call | solution.py:895
  39.4 1.6 %emit.1 = (f32[24,2,384]{2,1,0:T(2,128)}, f32[24,2,384]{2,1,0:T(2,128)}) custom-call(f32[2,3,48,128]{3,2,1,0:T(8,128)} %whole_step.1.tiled_ref), custom_call_target="tpu_custom_call" | custom-call | tf_op jit(solution)/shard_map/emit/pallas_call | solution.py:947

commit v5 on v4

--- a/solution.py
+++ b/solution.py
@@ -686,7 +686,7 @@
             await_block(8 * j + column)
         lat_step(flip_all(me, 8 * j) // 8)
 
-    lead = min(1, depth - 1)
+    lead = min(2, depth - 1)
     for j in range(1, depth):
         near_blocks(j)
     for j in range(depth + lead):

time: 41.2 us -> 41.2 us (level)
  no operation moved by 1% of the time
where the time goes in v5:
time: 41.2 us; the launch traced here: 41.1 us
  Pallas kernels  40.4 us (98%)
  between operations  0.64 us (2%)
    pallas_call x1, Pallas kernels, whole_step(): pl.pallas_call(functools.partial(step_kernel, count, mine * count), out_s...  38.8 us
    pallas_call x1, Pallas kernels, whole_step(): pl.pallas_call(emit_kernel, out_shape=(jax.ShapeDtypeStruct(state.shape,...  1.61 us

profile of v5, /device:TPU:0, one launch (start us, length us, event | category | flops | bytes accessed | tf_op | source)
XLA Modules:
  0.0 41.1 jit_solution(18259761423520894487)
XLA Ops:
  0.6 38.8 %whole_step.1.tiled_ref = f32[2,3,48,128]{3,2,1,0:T(8,128)} custom-call(bf16[4,768,2,384]{3,2,1,0:T(2,128)(2,1)} %members_hbm.1, f32[24,2,384]{2,1,0:T(2,128)} %state_hbm.1, f32[24,2,384]{2,1,0:T(2,128)} %cot_hbm.1, f32[3,3,2,128]{3,2,1,0:T(2,128)} %bitcast.2, f32[3,3,2,128]{3,2,1,0:T(2,128)} %wout_hbm.1, f32[1,128]{1,0:T(1,128)} %bitcast.3), custom_call_target="tpu_custom_call" | custom-call | tf_op jit(solution)/shard_map/whole_step/pallas_call | solution.py:895
  39.5 1.6 %emit.1 = (f32[24,2,384]{2,1,0:T(2,128)}, f32[24,2,384]{2,1,0:T(2,128)}) custom-call(f32[2,3,48,128]{3,2,1,0:T(8,128)} %whole_step.1.tiled_ref), custom_call_target="tpu_custom_call" | custom-call | tf_op jit(solution)/shard_map/emit/pallas_call | solution.py:947
